TPU v7x, 256 devices: a whole 4x4x8 slice. The times are simulated.
256 devices in a mesh: dp: 64 (over z, y, core), mp: 4 (over x).
Axes of the slice: x: 4, y: 4, z: 8, core: 2. Of those that a mesh axis runs over, the one named last changes fastest.
Arguments:
- patches: bfloat16 [131072, 1024], P('dp'), may hold values from -110 to 110
- dest_owner: int32 [8192], P('dp'), may hold values from 0 to 63, as said below
- dest_slot: int32 [8192], P('dp'), may hold values from 0 to 127
- packed_image: int32 [8192], P('dp'), may hold values from -1 to 15, as said below
- w_query: bfloat16 [1024, 1024], P(None, 'mp'), may hold values from -0.328125 to 0.328125
- w_key: bfloat16 [1024, 1024], P(None, 'mp'), may hold values from -1.9375 to 1.9375
- w_value: bfloat16 [1024, 1024], P(None, 'mp'), may hold values from -0.1875 to 0.1875
- w_out: bfloat16 [1024, 1024], P('mp'), may hold values from -0.1875 to 0.1875
Outputs:
- packed_out: bfloat16 [131072, 1024], P('dp', 'mp')
- pooled_out: bfloat16 [1024, 1024], P('dp', 'mp')
Inputs may be any that keep to these rules, and one draw needn't show every extreme that they name: dest_owner and dest_slot take the tiles of all indices of dp one to one onto the 128 tile slots of every packed sequence; each index of dp holds exactly 2 tiles for each packed sequence. `packed_image`: in every packed sequence the images 0, 1, 2 and so on lie on consecutive tile slots from slot 0 in the order of their numbers, each on 8 to 16 slots; fewer than 16 slots stay empty after the last image and hold -1.
All inputs are finite; a program needn't handle non-finite values.
Results may differ from a plain program's by a relative error of at most 0.0075.
Values may be sent and summed in bfloat16 or wider, within the bound.
No kernel may reach another device: no remote copies, remote signals or barrier semaphores. Data moves between devices by JAX's collectives and lax.ppermute only.
A program may use at most 128 MiB of HBM per device.

v0:
```python
import jax
import jax.numpy as jnp
from jax import lax
from jax.sharding import PartitionSpec as P

HEAD_DIM = 64
IMG_OWN = 16
EPSILON = 1e-06


def cut_along(shard, dim, length):
    lengths = shard.shape
    tiles = shard.reshape(*lengths[:dim], length, lengths[dim] // length, *lengths[dim + 1 :])
    return jnp.moveaxis(tiles, dim, 0)


def sent_and_summed(shard, axis, dim):
    length = lax.axis_size(axis)
    tiles = lax.all_to_all(cut_along(shard, dim, length), axis, 0, 0, tiled=True)
    return jnp.sum(tiles.astype(jnp.float32), axis=0)


def sent_to_all(shard, axis):
    copies = jnp.broadcast_to(shard, (lax.axis_size(axis), *shard.shape))
    return lax.all_to_all(copies, axis, split_axis=0, concat_axis=0, tiled=True)


def of_everyone(shard, axis):
    return sent_to_all(shard, axis).sum(axis=0)


def in_one(arrays, axis):
    line, at, outs = (jnp.concatenate([a.reshape(-1) for a in arrays]), 0, [])
    running = of_everyone(line, axis)
    for a in arrays:
        outs.append(running[at : at + a.size].reshape(a.shape))
        at += a.size
    return tuple(outs)


def normalize(rows):
    values = rows.astype(jnp.float32)
    centred = values - jnp.mean(values, axis=-1, keepdims=True)
    spread = jnp.mean(centred * centred, axis=-1, keepdims=True)
    return (centred * lax.rsqrt(spread + EPSILON)).astype(jnp.bfloat16)


def attend(queries, key_rows, values, allowed, present):
    scores = jnp.einsum(
        "qhd,khd->hqk", queries, key_rows, preferred_element_type=jnp.float32
    ) * HEAD_DIM ** (-0.5)
    masked = jnp.where(allowed[None], scores, -1e30)
    peak = jnp.max(masked, axis=-1, keepdims=True)
    raised = jnp.where(allowed[None], jnp.exp(scores - peak), 0.0)
    denominator = jnp.sum(raised, axis=-1, keepdims=True)
    denominator = jnp.where(present[None, :, None], denominator, 1.0)
    weights = (raised / denominator).astype(jnp.bfloat16)
    return jnp.einsum("hqk,khd->qhd", weights, values, preferred_element_type=jnp.float32).astype(
        jnp.bfloat16
    )


def whole_rows(queries, key_rows, values, segment, present):
    count_rows = queries.shape[0]
    block_rows = min(512, count_rows)

    def one_block(step_index):
        first_row = step_index * block_rows
        query_part = lax.dynamic_slice_in_dim(queries, first_row, block_rows, 0)
        segment_part = lax.dynamic_slice_in_dim(segment, first_row, block_rows, 0)
        live_rows = lax.dynamic_slice_in_dim(present, first_row, block_rows, 0)
        allowed = (segment_part[:, None] == segment[None, :]) & live_rows[:, None]
        return attend(query_part, key_rows, values, allowed, live_rows)

    outcome = lax.map(one_block, jnp.arange(count_rows // block_rows, dtype=jnp.int32))
    return outcome.reshape(count_rows, -1)


def on_device(patches, dest_owner, dest_slot, packed_image, w_query, w_key, w_value, w_out):
    senders = lax.axis_size("dp")
    splits = lax.axis_size("mp")
    slot_count = dest_owner.shape[0]
    per_owner = slot_count // senders
    tile_size = patches.shape[0] // slot_count
    full_width = patches.shape[1]
    part_width = full_width // splits
    numbers = jnp.arange(slot_count, dtype=jnp.int32)
    same_owner = dest_owner[:, None] == dest_owner[None, :]
    ranking = jnp.sum(
        (same_owner & (numbers[None, :] < numbers[:, None])).astype(jnp.int32), axis=1
    )
    position = dest_owner * per_owner + ranking
    picked = position[None, :] == numbers[:, None]
    ordering = jnp.sum(jnp.where(picked, numbers[None, :], 0), axis=1)
    slot_sent = jnp.sum(jnp.where(picked, dest_slot[None, :], 0), axis=1)
    got_slot = lax.all_to_all(slot_sent, "dp", split_axis=0, concat_axis=0, tiled=True)
    arrive = jnp.sum(jnp.where(got_slot[None, :] == numbers[:, None], numbers[None, :], 0), axis=1)
    tile_data = patches.reshape(slot_count, tile_size, full_width)
    column_start = lax.axis_index("mp") * part_width
    own_part = lax.dynamic_slice_in_dim(tile_data, column_start, part_width, 2)
    outgoing = jnp.take(own_part, ordering, axis=0).reshape(slot_count * tile_size, part_width)
    incoming = lax.all_to_all(outgoing, "dp", split_axis=0, concat_axis=0, tiled=True)
    own_cols = jnp.take(
        incoming.reshape(slot_count, tile_size, part_width), arrive, axis=0
    ).reshape(slot_count * tile_size, part_width)
    full_rows = lax.all_gather(own_cols, "mp", axis=1, tiled=True)
    count_rows = slot_count * tile_size
    segment = jnp.repeat(packed_image, tile_size)
    present = segment >= 0
    normed = normalize(full_rows)
    head_count = w_query.shape[1] // HEAD_DIM
    queries = (
        jnp.dot(normed, w_query, preferred_element_type=jnp.float32)
        .astype(jnp.bfloat16)
        .reshape(count_rows, head_count, HEAD_DIM)
    )
    key_rows = (
        jnp.dot(normed, w_key, preferred_element_type=jnp.float32)
        .astype(jnp.bfloat16)
        .reshape(count_rows, head_count, HEAD_DIM)
    )
    values = (
        jnp.dot(normed, w_value, preferred_element_type=jnp.float32)
        .astype(jnp.bfloat16)
        .reshape(count_rows, head_count, HEAD_DIM)
    )
    attended = whole_rows(queries, key_rows, values, segment, present)
    head_term = jnp.dot(attended, w_out, preferred_element_type=jnp.float32)
    summed = sent_and_summed(head_term.astype(jnp.bfloat16), "mp", 1)
    result_rows = jnp.where(present[:, None], own_cols.astype(jnp.float32) + summed, 0.0)
    packed_out = result_rows.astype(jnp.bfloat16)
    labels = jnp.arange(IMG_OWN, dtype=jnp.int32)
    member = (segment[None, :] == labels[:, None]).astype(jnp.float32)
    sums = jnp.dot(member, result_rows)
    image_rows = jnp.sum(member, axis=1)
    filled = image_rows > 0
    pooled = sums / jnp.maximum(image_rows, 1.0)[:, None]
    local_sum = jnp.sum(jnp.where(filled[:, None], pooled, 0.0), axis=0)
    local_count = jnp.sum(filled.astype(jnp.float32))
    grand_total, number = in_one((local_sum, local_count), "dp")
    centre = grand_total / number
    pooled_out = jnp.where(filled[:, None], pooled - centre[None, :], 0.0).astype(jnp.bfloat16)
    return (packed_out, pooled_out)


def solution(mesh):
    in_specs = (
        P("dp", None),
        P("dp"),
        P("dp"),
        P("dp"),
        P(None, "mp"),
        P(None, "mp"),
        P(None, "mp"),
        P("mp", None),
    )
    out_specs = (P("dp", "mp"), P("dp", "mp"))
    return jax.shard_map(
        on_device, mesh=mesh, in_specs=in_specs, out_specs=out_specs, check_vma=False
    )
```

profile of v0, /device:TPU:1, one launch (start us, length us, event | category | flops | bytes accessed | tf_op | source)
XLA Modules:
  0.0 322.7 jit_solution(6817620751752851636)
XLA Ops:
  10.3 13.1 %all-to-all-start.1 = ((s32[64,2,1]{1,2,0:T(1,128)}), s32[64,2,1]{1,2,0:T(1,128)S(1)}, u32[]{:S(2)}, u32[]{:S(2)}) async-start(s32[64,2,1]{1,2,0:T(1,128)} %bitcast), calls=%async_computation.1 | async-start | bytes 65536 | tf_op jit(solution)/shard_map/all_to_all | solution.py:96
  26.6 6.2 %all-to-all-done.1 = s32[64,2,1]{1,2,0:T(1,128)S(1)} async-done(((s32[64,2,1]{1,2,0:T(1,128)}), s32[64,2,1]{1,2,0:T(1,128)S(1)}, u32[]{:S(2)}, u32[]{:S(2)}) %all-to-all-start.1) | async-done | bytes 544 | tf_op jit(solution)/shard_map/all_to_all | solution.py:96
  32.8 4.7 %all-to-all-start = ((bf16[64,32,256]{2,1,0:T(8,128)(2,1)}), bf16[64,32,256]{2,1,0:T(8,128)(2,1)S(1)}, u32[]{:S(2)}, u32[]{:S(2)}) async-start(bf16[64,32,256]{2,1,0:T(8,128)(2,1)} %bitcast.2), calls=%async_computation | async-start | bytes 2097152 | tf_op jit(solution)/shard_map/all_to_all | solution.py:102
  39.2 26.7 %all-to-all-done = bf16[64,32,256]{2,1,0:T(8,128)(2,1)S(1)} async-done(((bf16[64,32,256]{2,1,0:T(8,128)(2,1)}), bf16[64,32,256]{2,1,0:T(8,128)(2,1)S(1)}, u32[]{:S(2)}, u32[]{:S(2)}) %all-to-all-start) | async-done | bytes 1048608 | tf_op jit(solution)/shard_map/all_to_all | solution.py:102
  67.9 49.4 %all-gather.2.cloned.1.call-done = bf16[2048,1024]{1,0:T(8,128)(2,1)} async-done(((bf16[2048,256]{1,0:T(8,128)(2,1)}), bf16[2048,1024]{1,0:T(8,128)(2,1)}) %all-gather.2.cloned.1.call-update) | async-done | bytes 4194320 | tf_op jit(solution)/shard_map/all_gather | solution.py:106
  117.4 3.0 convert_reduce_fusion
  123.4 2.3 convolution_convert_fusion.3
  125.7 2.3 convolution_convert_fusion.2
  130.3 98.7 %while.11 = (s32[]{:T(128)}, bf16[4,512,4,64]{1,3,2,0:T(8,128)(2,1)S(1)}, s32[4]{0:T(128)S(1)}, s32[2048]{0:T(1024)S(1)}, pred[2048]{0:T(1024)(128)(4,1)S(1)}, /...) while((s32[]{:T(128)}, ...), condition=%wide.region_9.11_spmd.clone, body=%wide.region_6.0_spmd.clone.sunk | while | flops 1646399488 | bytes 40707776 | solution.py:75
  132.8 13.4 %fusion.69 = (f32[4,512]{1,0:T(4,128)S(1)}, f32[4,512,2048]{2,1,0:T(8,128)}) fusion(pred[512,2048]{1,0:T(8,128)(4,1)S(1)} %compare_and_fusion.4, bf16[2048,4,64]{0,2,1:T(8,128)(2,1)} %get-tuple-element.197, bf16[2048,4,64]{0,2,1:T(8,128)(2,1)} %get-tuple-element.196, s32[]{:T(128)S(6)} %select_n.104), kind=kOutput, calls=%fused_computation.75.clone.1 | convolution fusion | flops 1098909696 | bytes 21505024 | tf_op jit(solution)/shard_map/while/body/eval_jaxpr/sub | solution.py:54
  146.2 8.7 %fusion.70 = bf16[4,512,4,64]{1,3,2,0:T(8,128)(2,1)S(1)} fusion(bf16[4,512,4,64]{1,3,2,0:T(8,128)(2,1)S(1)} %get-tuple-element.179, s32[]{:T(128)} %get-tuple-element.178, bf16[2048,4,64]{0,2,1:T(8,128)(2,1)} %get-tuple-element.198, f32[4,512,2048]{2,1,0:T(8,128)} %get-tuple-element.163, f32[4,512]{1,0:T(4,128)S(1)} %broadcast_select_fusion.4), kind=kOutput, calls=%fused_computation.17.clone.1 | convolution fusion | flops 545390592 | bytes 18096132 | tf_op jit(solution)/shard_map/while/body/eval_jaxpr/hqk,khd->qhd/dot_general | solution.py:58
  157.4 13.4 %fusion.69 = (f32[4,512]{1,0:T(4,128)S(1)}, f32[4,512,2048]{2,1,0:T(8,128)}) fusion(pred[512,2048]{1,0:T(8,128)(4,1)S(1)} %compare_and_fusion.4, bf16[2048,4,64]{0,2,1:T(8,128)(2,1)} %get-tuple-element.197, bf16[2048,4,64]{0,2,1:T(8,128)(2,1)} %get-tuple-element.196, s32[]{:T(128)S(6)} %select_n.104), kind=kOutput, calls=%fused_computation.75.clone.1 | convolution fusion | flops 1098909696 | bytes 21505024 | tf_op jit(solution)/shard_map/while/body/eval_jaxpr/sub | solution.py:54
  170.9 8.7 %fusion.70 = bf16[4,512,4,64]{1,3,2,0:T(8,128)(2,1)S(1)} fusion(bf16[4,512,4,64]{1,3,2,0:T(8,128)(2,1)S(1)} %get-tuple-element.179, s32[]{:T(128)} %get-tuple-element.178, bf16[2048,4,64]{0,2,1:T(8,128)(2,1)} %get-tuple-element.198, f32[4,512,2048]{2,1,0:T(8,128)} %get-tuple-element.163, f32[4,512]{1,0:T(4,128)S(1)} %broadcast_select_fusion.4), kind=kOutput, calls=%fused_computation.17.clone.1 | convolution fusion | flops 545390592 | bytes 18096132 | tf_op jit(solution)/shard_map/while/body/eval_jaxpr/hqk,khd->qhd/dot_general | solution.py:58
  182.1 13.5 %fusion.69 = (f32[4,512]{1,0:T(4,128)S(1)}, f32[4,512,2048]{2,1,0:T(8,128)}) fusion(pred[512,2048]{1,0:T(8,128)(4,1)S(1)} %compare_and_fusion.4, bf16[2048,4,64]{0,2,1:T(8,128)(2,1)} %get-tuple-element.197, bf16[2048,4,64]{0,2,1:T(8,128)(2,1)} %get-tuple-element.196, s32[]{:T(128)S(6)} %select_n.104), kind=kOutput, calls=%fused_computation.75.clone.1 | convolution fusion | flops 1098909696 | bytes 21505024 | tf_op jit(solution)/shard_map/while/body/eval_jaxpr/sub | solution.py:54
  195.6 8.7 %fusion.70 = bf16[4,512,4,64]{1,3,2,0:T(8,128)(2,1)S(1)} fusion(bf16[4,512,4,64]{1,3,2,0:T(8,128)(2,1)S(1)} %get-tuple-element.179, s32[]{:T(128)} %get-tuple-element.178, bf16[2048,4,64]{0,2,1:T(8,128)(2,1)} %get-tuple-element.198, f32[4,512,2048]{2,1,0:T(8,128)} %get-tuple-element.163, f32[4,512]{1,0:T(4,128)S(1)} %broadcast_select_fusion.4), kind=kOutput, calls=%fused_computation.17.clone.1 | convolution fusion | flops 545390592 | bytes 18096132 | tf_op jit(solution)/shard_map/while/body/eval_jaxpr/hqk,khd->qhd/dot_general | solution.py:58
  206.8 13.4 %fusion.69 = (f32[4,512]{1,0:T(4,128)S(1)}, f32[4,512,2048]{2,1,0:T(8,128)}) fusion(pred[512,2048]{1,0:T(8,128)(4,1)S(1)} %compare_and_fusion.4, bf16[2048,4,64]{0,2,1:T(8,128)(2,1)} %get-tuple-element.197, bf16[2048,4,64]{0,2,1:T(8,128)(2,1)} %get-tuple-element.196, s32[]{:T(128)S(6)} %select_n.104), kind=kOutput, calls=%fused_computation.75.clone.1 | convolution fusion | flops 1098909696 | bytes 21505024 | tf_op jit(solution)/shard_map/while/body/eval_jaxpr/sub | solution.py:54
  220.2 8.7 %fusion.70 = bf16[4,512,4,64]{1,3,2,0:T(8,128)(2,1)S(1)} fusion(bf16[4,512,4,64]{1,3,2,0:T(8,128)(2,1)S(1)} %get-tuple-element.179, s32[]{:T(128)} %get-tuple-element.178, bf16[2048,4,64]{0,2,1:T(8,128)(2,1)} %get-tuple-element.198, f32[4,512,2048]{2,1,0:T(8,128)} %get-tuple-element.163, f32[4,512]{1,0:T(4,128)S(1)} %broadcast_select_fusion.4), kind=kOutput, calls=%fused_computation.17.clone.1 | convolution fusion | flops 545390592 | bytes 18096132 | tf_op jit(solution)/shard_map/while/body/eval_jaxpr/hqk,khd->qhd/dot_general | solution.py:58
  230.1 3.3 %convolution_convert_fusion = bf16[2048,1024]{0,1:T(8,128)(2,1)} fusion(bf16[2048,256]{0,1:T(8,128)(2,1)S(1)} %bitcast.50, bf16[256,1024]{1,0:T(8,128)(2,1)S(1)} %copy-done), kind=kOutput, calls=%fused_computation.33 | convolution fusion | flops 1075838976 | bytes 5767168 | tf_op jit(solution)/shard_map/dot_general | solution.py:128
  233.4 5.0 %all-to-all-start.2 = ((bf16[4,2048,256]{1,2,0:T(8,128)(2,1)}), bf16[4,2048,256]{1,2,0:T(8,128)(2,1)}, u32[]{:S(2)}, u32[]{:S(2)}) async-start(bf16[4,2048,256]{1,2,0:T(8,128)(2,1)} %bitcast.47), calls=%async_computation.2 | async-start | bytes 8388608 | tf_op jit(solution)/shard_map/all_to_all | solution.py:19
  240.5 44.8 %all-to-all-done.2 = bf16[4,2048,256]{1,2,0:T(8,128)(2,1)} async-done(((bf16[4,2048,256]{1,2,0:T(8,128)(2,1)}), bf16[4,2048,256]{1,2,0:T(8,128)(2,1)}, u32[]{:S(2)}, u32[]{:S(2)}) %all-to-all-start.2) | async-done | bytes 4194336 | tf_op jit(solution)/shard_map/all_to_all | solution.py:19
  285.3 3.2 %convert_reduce_fusion.1 = f32[2048,256]{0,1:T(8,128)S(1)} fusion(bf16[4,2048,256]{1,2,0:T(8,128)(2,1)} %all-to-all-done.2), kind=kLoop, calls=%fused_computation.32 | loop fusion | flops 3670016 | bytes 6291456 | tf_op jit(solution)/shard_map/reduce_sum | solution.py:20
  290.4 12.9 %all-to-all-start.3 = ((f32[64,1,257]{2,1,0:T(1,128)}), f32[64,1,257]{2,1,0:T(1,128)S(1)}, u32[]{:S(2)}, u32[]{:S(2)}) async-start(f32[64,1,257]{2,1,0:T(1,128)} %broadcast_in_dim.134), calls=%async_computation.3 | async-start | bytes 196608 | tf_op jit(solution)/shard_map/all_to_all | solution.py:25
  303.3 2.5 fusion.34
  308.1 5.8 %all-to-all-done.3 = f32[64,1,257]{2,1,0:T(1,128)S(1)} async-done(((f32[64,1,257]{2,1,0:T(1,128)}), f32[64,1,257]{2,1,0:T(1,128)S(1)}, u32[]{:S(2)}, u32[]{:S(2)}) %all-to-all-start.3) | async-done | bytes 65824 | tf_op jit(solution)/shard_map/all_to_all | solution.py:25
  (89 shorter events, 31.4 us)
Async XLA Ops:
  7.2 222.9 %copy-start = (bf16[256,1024]{1,0:T(8,128)(2,1)S(1)}, bf16[256,1024]{1,0:T(8,128)(2,1)}, u32[]{:S(2)}) copy-start(bf16[256,1024]{1,0:T(8,128)(2,1)} %param.19) | copy-start | bytes 1572868
  10.3 22.6 %all-to-all-start.1 = ((s32[64,2,1]{1,2,0:T(1,128)}), s32[64,2,1]{1,2,0:T(1,128)S(1)}, u32[]{:S(2)}, u32[]{:S(2)}) async-start(s32[64,2,1]{1,2,0:T(1,128)} %bitcast), calls=%async_computation.1 | async-start | bytes 65536 | tf_op jit(solution)/shard_map/all_to_all | solution.py:96
  26.6 41.1 %copy-start.4 = (s32[128]{0:T(128)S(1)}, s32[128]{0:T(128)}, u32[]{:S(2)}) copy-start(s32[128]{0:T(128)} %param.15) | copy-start | bytes 1540
  32.8 33.1 %all-to-all-start = ((bf16[64,32,256]{2,1,0:T(8,128)(2,1)}), bf16[64,32,256]{2,1,0:T(8,128)(2,1)S(1)}, u32[]{:S(2)}, u32[]{:S(2)}) async-start(bf16[64,32,256]{2,1,0:T(8,128)(2,1)} %bitcast.2), calls=%async_computation | async-start | bytes 2097152 | tf_op jit(solution)/shard_map/all_to_all | solution.py:102
  37.6 79.8 %all-gather.2.cloned.1.call-start = ((), (), s32[]{:S(2)}) async-start(), calls=%async_computation.4 | async-start | bytes 5242880 | tf_op jit(solution)/shard_map/all_gather | solution.py:106
  117.4 3.4 %copy-start.1 = (bf16[2048,1024]{1,0:T(8,128)(2,1)S(1)}, bf16[2048,1024]{1,0:T(8,128)(2,1)}, u32[]{:S(2)}) copy-start(bf16[2048,1024]{1,0:T(8,128)(2,1)} %all-gather.2.cloned.1.call-done) | copy-start | bytes 12582916
  122.2 1.1 copy-start.5
  123.4 2.3 copy-start.6
  125.7 2.3 copy-start.7
  233.4 5.7 %copy-start.2 = (bf16[128,16,256]{2,1,0:T(8,128)(2,1)S(1)}, bf16[128,16,256]{2,1,0:T(8,128)(2,1)}, u32[]{:S(2)}) copy-start(bf16[128,16,256]{2,1,0:T(8,128)(2,1)} %broadcast_select_fusion.1) | copy-start | bytes 3145732
  233.4 51.9 %all-to-all-start.2 = ((bf16[4,2048,256]{1,2,0:T(8,128)(2,1)}), bf16[4,2048,256]{1,2,0:T(8,128)(2,1)}, u32[]{:S(2)}, u32[]{:S(2)}) async-start(bf16[4,2048,256]{1,2,0:T(8,128)(2,1)} %bitcast.47), calls=%async_computation.2 | async-start | bytes 8388608 | tf_op jit(solution)/shard_map/all_to_all | solution.py:19
  285.3 3.3 %copy-start.3 = (bf16[2048,256]{0,1:T(8,128)(2,1)S(1)}, bf16[2048,256]{0,1:T(8,128)(2,1)}, u32[]{:S(2)}) copy-start(bf16[2048,256]{0,1:T(8,128)(2,1)} %copy.23) | copy-start | bytes 3145732
  290.4 23.5 %all-to-all-start.3 = ((f32[64,1,257]{2,1,0:T(1,128)}), f32[64,1,257]{2,1,0:T(1,128)S(1)}, u32[]{:S(2)}, u32[]{:S(2)}) async-start(f32[64,1,257]{2,1,0:T(1,128)} %broadcast_in_dim.134), calls=%async_computation.3 | async-start | bytes 196608 | tf_op jit(solution)/shard_map/all_to_all | solution.py:25
Sparse Core Ops, SparseCore 0:
  67.9 49.4 all-gather.1
where the time goes:
time: 323 us
  waiting for transfers between devices  133 us (41%)
  matrix products  99.3 us (31%)
  starting transfers between devices  35.8 us (11%)
  other arithmetic  22.8 us (7%)
  local copies, waits for them, and re-layouts  14.6 us (5%)
  between operations  14.3 us (4%)
    sub x4, matrix products, attend(): raised = jnp.where(allowed[None], jnp.exp(scores - peak), 0.0)  53.8 us
    all_gather x1, waiting for transfers between devices, on_device(): full_rows = lax.all_gather(own_cols, 'mp', axis=1, tiled=True)  49.4 us
    all_to_all x1, waiting for transfers between devices, sent_and_summed(): lax.all_to_all(cut_along(shard, dim, length), axis, 0, 0, tiled=True)  44.8 us
    dot_general x4, matrix products, attend(): jnp.einsum('hqk,khd->qhd', weights, values, preferred_element_type=jnp.fl...  34.9 us
    all_to_all x1, waiting for transfers between devices, on_device(): lax.all_to_all(outgoing, 'dp', split_axis=0, concat_axis=0, tiled=True)  26.7 us
    all_to_all x1, starting transfers between devices, on_device(): lax.all_to_all(slot_sent, 'dp', split_axis=0, concat_axis=0, tiled=True)  13.1 us
    all_to_all x1, starting transfers between devices, sent_to_all(): return lax.all_to_all(copies, axis, split_axis=0, concat_axis=0, tiled=True)  12.9 us
  transfers between devices with their start and end apart: 5, of which 5 were waited for; matrix products, arithmetic and copies ran while one was open for 4% of the time, Pallas kernels for 0%

commit v1 on v0

--- a/solution.py
+++ b/solution.py
@@ -103,7 +103,24 @@
     own_cols = jnp.take(
         incoming.reshape(slot_count, tile_size, part_width), arrive, axis=0
     ).reshape(slot_count * tile_size, part_width)
-    full_rows = lax.all_gather(own_cols, "mp", axis=1, tiled=True)
+    size, position_2, rows_2 = (lax.axis_size("mp"), lax.axis_index("mp"), own_cols.shape[1])
+    upward = [(i, (i + 1) % size) for i in range(size)]
+    backward = [(i, (i - 1) % size) for i in range(size)]
+    out = jnp.zeros((*own_cols.shape[:1], size * rows_2, *own_cols.shape[1 + 1 :]), own_cols.dtype)
+    out = lax.dynamic_update_slice_in_dim(out, own_cols, position_2 * rows_2, axis=1)
+    from_left = from_right = own_cols
+    half = size // 2
+    for step in range(1, half + 1):
+        from_left = lax.ppermute(from_left, "mp", upward)
+        out = lax.dynamic_update_slice_in_dim(
+            out, from_left, (position_2 - step) % size * rows_2, axis=1
+        )
+        if step < size - half:
+            from_right = lax.ppermute(from_right, "mp", backward)
+            out = lax.dynamic_update_slice_in_dim(
+                out, from_right, (position_2 + step) % size * rows_2, axis=1
+            )
+    full_rows = out
     count_rows = slot_count * tile_size
     segment = jnp.repeat(packed_image, tile_size)
     present = segment >= 0

time: 323 us -> 304 us (0.941)
  between operations: 14.3 us -> 0.99 us
  waiting for transfers between devices: 133 us -> 126 us
  other arithmetic: 22.8 us -> 19.5 us
    all_gather x1 -> x0, waiting for transfers between devices: 49.4 us -> none  [on_device(): full_rows = lax.all_gather(own_cols, 'mp', axis=1, tiled=True)]
    ppermute x0 -> x3, waiting for transfers between devices: none -> 43.7 us  [the longest x2 43.7 us: on_device(): from_left = lax.ppermute(from_left, 'mp', upward)]
  transfers between devices with their start and end apart: 5 -> 7, of which waited for: 5 -> 6; matrix products, arithmetic and copies ran while one was open for 4% -> 5% of each run, Pallas kernels for 0% -> 0%
where the time goes in v1:
time: 304 us; the launch traced here: 303 us
  waiting for transfers between devices  126 us (41%)
  matrix products  99.5 us (33%)
  starting transfers between devices  36.7 us (12%)
  other arithmetic  19.5 us (6%)
  local copies, waits for them, and re-layouts  17.3 us (6%)
    sub x4, matrix products, attend(): raised = jnp.where(allowed[None], jnp.exp(scores - peak), 0.0)  54 us
    all_to_all x1, waiting for transfers between devices, sent_and_summed(): lax.all_to_all(cut_along(shard, dim, length), axis, 0, 0, tiled=True)  43.9 us
    ppermute x2, waiting for transfers between devices, on_device(): from_left = lax.ppermute(from_left, 'mp', upward)  43.7 us
    dot_general x4, matrix products, attend(): jnp.einsum('hqk,khd->qhd', weights, values, preferred_element_type=jnp.fl...  34.9 us
    all_to_all x1, waiting for transfers between devices, on_device(): lax.all_to_all(outgoing, 'dp', split_axis=0, concat_axis=0, tiled=True)  26.8 us
    all_to_all x1, starting transfers between devices, on_device(): lax.all_to_all(slot_sent, 'dp', split_axis=0, concat_axis=0, tiled=True)  13.1 us
    all_to_all x1, starting transfers between devices, sent_to_all(): return lax.all_to_all(copies, axis, split_axis=0, concat_axis=0, tiled=True)  11 us
    all_to_all x1, waiting for transfers between devices, on_device(): lax.all_to_all(slot_sent, 'dp', split_axis=0, concat_axis=0, tiled=True)  6.21 us
  transfers between devices with their start and end apart: 7, of which 6 were waited for; matrix products, arithmetic and copies ran while one was open for 5% of the time, Pallas kernels for 0%

profile of v1, /device:TPU:1, one launch (start us, length us, event | category | flops | bytes accessed | tf_op | source)
XLA Modules:
  0.0 303.1 jit_solution(7700531738590683708)
XLA Ops:
  3.7 13.1 %all-to-all-start.1 = ((s32[64,2,1]{1,2,0:T(1,128)}), s32[64,2,1]{1,2,0:T(1,128)S(1)}, u32[]{:S(2)}, u32[]{:S(2)}) async-start(s32[64,2,1]{1,2,0:T(1,128)} %bitcast), calls=%async_computation.1 | async-start | bytes 65536 | tf_op jit(solution)/shard_map/all_to_all | solution.py:96
  20.1 6.2 %all-to-all-done.1 = s32[64,2,1]{1,2,0:T(1,128)S(1)} async-done(((s32[64,2,1]{1,2,0:T(1,128)}), s32[64,2,1]{1,2,0:T(1,128)S(1)}, u32[]{:S(2)}, u32[]{:S(2)}) %all-to-all-start.1) | async-done | bytes 544 | tf_op jit(solution)/shard_map/all_to_all | solution.py:96
  26.3 4.7 %all-to-all-start = ((bf16[64,32,256]{2,1,0:T(8,128)(2,1)}), bf16[64,32,256]{2,1,0:T(8,128)(2,1)S(1)}, u32[]{:S(2)}, u32[]{:S(2)}) async-start(bf16[64,32,256]{2,1,0:T(8,128)(2,1)} %bitcast.2), calls=%async_computation | async-start | bytes 2097152 | tf_op jit(solution)/shard_map/all_to_all | solution.py:102
  32.6 26.8 %all-to-all-done = bf16[64,32,256]{2,1,0:T(8,128)(2,1)S(1)} async-done(((bf16[64,32,256]{2,1,0:T(8,128)(2,1)}), bf16[64,32,256]{2,1,0:T(8,128)(2,1)S(1)}, u32[]{:S(2)}, u32[]{:S(2)}) %all-to-all-start) | async-done | bytes 1048608 | tf_op jit(solution)/shard_map/all_to_all | solution.py:102
  63.0 22.1 %collective-permute-done = bf16[2048,256]{1,0:T(8,128)(2,1)S(1)} collective-permute-done((bf16[2048,256]{1,0:T(8,128)(2,1)S(1)}, bf16[2048,256]{1,0:T(8,128)(2,1)S(1)}, u32[]{:S(2)}, u32[]{:S(2)}) %collective-permute-start) | collective-permute-done | bytes 1048608 | tf_op jit(solution)/shard_map/ppermute | solution.py:114
  87.6 21.5 %collective-permute-done.2 = bf16[2048,256]{1,0:T(8,128)(2,1)} collective-permute-done((bf16[2048,256]{1,0:T(8,128)(2,1)S(1)}, bf16[2048,256]{1,0:T(8,128)(2,1)}, u32[]{:S(2)}, u32[]{:S(2)}) %collective-permute-start.2) | collective-permute-done | bytes 1048608 | tf_op jit(solution)/shard_map/ppermute | solution.py:114
  113.7 2.3 convolution_convert_fusion.3
  116.1 2.3 convolution_convert_fusion.2
  120.6 98.4 %while.11 = (s32[]{:T(128)}, bf16[4,512,4,64]{1,3,2,0:T(8,128)(2,1)S(1)}, s32[4]{0:T(128)S(1)}, s32[2048]{0:T(1024)S(1)}, pred[2048]{0:T(1024)(128)(4,1)S(1)}, /...) while((s32[]{:T(128)}, ...), condition=%wide.region_9.11_spmd.clone, body=%wide.region_6.10_spmd.clone.sunk | while | flops 1646399488 | bytes 40707776 | solution.py:75
  123.0 13.5 %fusion.69 = (f32[4,512]{1,0:T(4,128)S(1)}, f32[4,512,2048]{2,1,0:T(8,128)}) fusion(pred[512,2048]{1,0:T(8,128)(4,1)S(1)} %compare_and_fusion.4, bf16[2048,4,64]{0,2,1:T(8,128)(2,1)} %get-tuple-element.197, bf16[2048,4,64]{0,2,1:T(8,128)(2,1)} %get-tuple-element.196, s32[]{:T(128)S(6)} %select_n.135), kind=kOutput, calls=%fused_computation.79.clone.1 | convolution fusion | flops 1098909696 | bytes 21505024 | tf_op jit(solution)/shard_map/while/body/eval_jaxpr/sub | solution.py:54
  136.4 8.7 %fusion.70 = bf16[4,512,4,64]{1,3,2,0:T(8,128)(2,1)S(1)} fusion(bf16[4,512,4,64]{1,3,2,0:T(8,128)(2,1)S(1)} %get-tuple-element.179, s32[]{:T(128)} %get-tuple-element.178, bf16[2048,4,64]{0,2,1:T(8,128)(2,1)} %get-tuple-element.198, f32[4,512,2048]{2,1,0:T(8,128)} %get-tuple-element.163, f32[4,512]{1,0:T(4,128)S(1)} %broadcast_select_fusion.4), kind=kOutput, calls=%fused_computation.17.clone.1 | convolution fusion | flops 545390592 | bytes 18096132 | tf_op jit(solution)/shard_map/while/body/eval_jaxpr/hqk,khd->qhd/dot_general | solution.py:58
  147.5 13.6 %fusion.69 = (f32[4,512]{1,0:T(4,128)S(1)}, f32[4,512,2048]{2,1,0:T(8,128)}) fusion(pred[512,2048]{1,0:T(8,128)(4,1)S(1)} %compare_and_fusion.4, bf16[2048,4,64]{0,2,1:T(8,128)(2,1)} %get-tuple-element.197, bf16[2048,4,64]{0,2,1:T(8,128)(2,1)} %get-tuple-element.196, s32[]{:T(128)S(6)} %select_n.135), kind=kOutput, calls=%fused_computation.79.clone.1 | convolution fusion | flops 1098909696 | bytes 21505024 | tf_op jit(solution)/shard_map/while/body/eval_jaxpr/sub | solution.py:54
  161.1 8.7 %fusion.70 = bf16[4,512,4,64]{1,3,2,0:T(8,128)(2,1)S(1)} fusion(bf16[4,512,4,64]{1,3,2,0:T(8,128)(2,1)S(1)} %get-tuple-element.179, s32[]{:T(128)} %get-tuple-element.178, bf16[2048,4,64]{0,2,1:T(8,128)(2,1)} %get-tuple-element.198, f32[4,512,2048]{2,1,0:T(8,128)} %get-tuple-element.163, f32[4,512]{1,0:T(4,128)S(1)} %broadcast_select_fusion.4), kind=kOutput, calls=%fused_computation.17.clone.1 | convolution fusion | flops 545390592 | bytes 18096132 | tf_op jit(solution)/shard_map/while/body/eval_jaxpr/hqk,khd->qhd/dot_general | solution.py:58
  172.2 13.5 %fusion.69 = (f32[4,512]{1,0:T(4,128)S(1)}, f32[4,512,2048]{2,1,0:T(8,128)}) fusion(pred[512,2048]{1,0:T(8,128)(4,1)S(1)} %compare_and_fusion.4, bf16[2048,4,64]{0,2,1:T(8,128)(2,1)} %get-tuple-element.197, bf16[2048,4,64]{0,2,1:T(8,128)(2,1)} %get-tuple-element.196, s32[]{:T(128)S(6)} %select_n.135), kind=kOutput, calls=%fused_computation.79.clone.1 | convolution fusion | flops 1098909696 | bytes 21505024 | tf_op jit(solution)/shard_map/while/body/eval_jaxpr/sub | solution.py:54
  185.7 8.7 %fusion.70 = bf16[4,512,4,64]{1,3,2,0:T(8,128)(2,1)S(1)} fusion(bf16[4,512,4,64]{1,3,2,0:T(8,128)(2,1)S(1)} %get-tuple-element.179, s32[]{:T(128)} %get-tuple-element.178, bf16[2048,4,64]{0,2,1:T(8,128)(2,1)} %get-tuple-element.198, f32[4,512,2048]{2,1,0:T(8,128)} %get-tuple-element.163, f32[4,512]{1,0:T(4,128)S(1)} %broadcast_select_fusion.4), kind=kOutput, calls=%fused_computation.17.clone.1 | convolution fusion | flops 545390592 | bytes 18096132 | tf_op jit(solution)/shard_map/while/body/eval_jaxpr/hqk,khd->qhd/dot_general | solution.py:58
  196.8 13.4 %fusion.69 = (f32[4,512]{1,0:T(4,128)S(1)}, f32[4,512,2048]{2,1,0:T(8,128)}) fusion(pred[512,2048]{1,0:T(8,128)(4,1)S(1)} %compare_and_fusion.4, bf16[2048,4,64]{0,2,1:T(8,128)(2,1)} %get-tuple-element.197, bf16[2048,4,64]{0,2,1:T(8,128)(2,1)} %get-tuple-element.196, s32[]{:T(128)S(6)} %select_n.135), kind=kOutput, calls=%fused_computation.79.clone.1 | convolution fusion | flops 1098909696 | bytes 21505024 | tf_op jit(solution)/shard_map/while/body/eval_jaxpr/sub | solution.py:54
  210.3 8.7 %fusion.70 = bf16[4,512,4,64]{1,3,2,0:T(8,128)(2,1)S(1)} fusion(bf16[4,512,4,64]{1,3,2,0:T(8,128)(2,1)S(1)} %get-tuple-element.179, s32[]{:T(128)} %get-tuple-element.178, bf16[2048,4,64]{0,2,1:T(8,128)(2,1)} %get-tuple-element.198, f32[4,512,2048]{2,1,0:T(8,128)} %get-tuple-element.163, f32[4,512]{1,0:T(4,128)S(1)} %broadcast_select_fusion.4), kind=kOutput, calls=%fused_computation.17.clone.1 | convolution fusion | flops 545390592 | bytes 18096132 | tf_op jit(solution)/shard_map/while/body/eval_jaxpr/hqk,khd->qhd/dot_general | solution.py:58
  220.1 3.3 %convolution_convert_fusion = bf16[2048,1024]{0,1:T(8,128)(2,1)} fusion(bf16[2048,256]{0,1:T(8,128)(2,1)S(1)} %bitcast.52, bf16[256,1024]{1,0:T(8,128)(2,1)S(1)} %copy-done), kind=kOutput, calls=%fused_computation.33 | convolution fusion | flops 1075838976 | bytes 5767168 | tf_op jit(solution)/shard_map/dot_general | solution.py:145
  223.4 5.0 %all-to-all-start.2 = ((bf16[4,2048,256]{1,2,0:T(8,128)(2,1)}), bf16[4,2048,256]{1,2,0:T(8,128)(2,1)}, u32[]{:S(2)}, u32[]{:S(2)}) async-start(bf16[4,2048,256]{1,2,0:T(8,128)(2,1)} %bitcast.47), calls=%async_computation.2 | async-start | bytes 8388608 | tf_op jit(solution)/shard_map/all_to_all | solution.py:19
  230.6 43.9 %all-to-all-done.2 = bf16[4,2048,256]{1,2,0:T(8,128)(2,1)} async-done(((bf16[4,2048,256]{1,2,0:T(8,128)(2,1)}), bf16[4,2048,256]{1,2,0:T(8,128)(2,1)}, u32[]{:S(2)}, u32[]{:S(2)}) %all-to-all-start.2) | async-done | bytes 4194336 | tf_op jit(solution)/shard_map/all_to_all | solution.py:19
  274.5 3.2 %convert_reduce_fusion.1 = f32[2048,256]{0,1:T(8,128)S(1)} fusion(bf16[4,2048,256]{1,2,0:T(8,128)(2,1)} %all-to-all-done.2), kind=kLoop, calls=%fused_computation.32 | loop fusion | flops 3670016 | bytes 6291456 | tf_op jit(solution)/shard_map/reduce_sum | solution.py:20
  279.6 11.0 %all-to-all-start.3 = ((f32[64,1,257]{2,1,0:T(1,128)}), f32[64,1,257]{2,1,0:T(1,128)S(1)}, u32[]{:S(2)}, u32[]{:S(2)}) async-start(f32[64,1,257]{2,1,0:T(1,128)} %broadcast_in_dim.138), calls=%async_computation.3 | async-start | bytes 196608 | tf_op jit(solution)/shard_map/all_to_all | solution.py:25
  290.6 2.5 fusion.34
  295.4 5.8 %all-to-all-done.3 = f32[64,1,257]{2,1,0:T(1,128)S(1)} async-done(((f32[64,1,257]{2,1,0:T(1,128)}), f32[64,1,257]{2,1,0:T(1,128)S(1)}, u32[]{:S(2)}, u32[]{:S(2)}) %all-to-all-start.3) | async-done | bytes 65824 | tf_op jit(solution)/shard_map/all_to_all | solution.py:25
  (99 shorter events, 36.6 us)
Async XLA Ops:
  0.6 219.5 %copy-start = (bf16[256,1024]{1,0:T(8,128)(2,1)S(1)}, bf16[256,1024]{1,0:T(8,128)(2,1)}, u32[]{:S(2)}) copy-start(bf16[256,1024]{1,0:T(8,128)(2,1)} %param.19) | copy-start | bytes 1572868
  3.7 22.6 %all-to-all-start.1 = ((s32[64,2,1]{1,2,0:T(1,128)}), s32[64,2,1]{1,2,0:T(1,128)S(1)}, u32[]{:S(2)}, u32[]{:S(2)}) async-start(s32[64,2,1]{1,2,0:T(1,128)} %bitcast), calls=%async_computation.1 | async-start | bytes 65536 | tf_op jit(solution)/shard_map/all_to_all | solution.py:96
  18.9 66.3 %copy-start.5 = (s32[128]{0:T(128)S(1)}, s32[128]{0:T(128)}, u32[]{:S(2)}) copy-start(s32[128]{0:T(128)} %param.15) | copy-start | bytes 1540
  26.3 33.1 %all-to-all-start = ((bf16[64,32,256]{2,1,0:T(8,128)(2,1)}), bf16[64,32,256]{2,1,0:T(8,128)(2,1)S(1)}, u32[]{:S(2)}, u32[]{:S(2)}) async-start(bf16[64,32,256]{2,1,0:T(8,128)(2,1)} %bitcast.2), calls=%async_computation | async-start | bytes 2097152 | tf_op jit(solution)/shard_map/all_to_all | solution.py:102
  60.2 26.0 %copy-start.1 = (bf16[128,16,256]{2,1,0:T(8,128)(2,1)}, bf16[128,16,256]{2,1,0:T(8,128)(2,1)S(1)}, u32[]{:S(2)}) copy-start(bf16[128,16,256]{2,1,0:T(8,128)(2,1)S(1)} %broadcast_select_fusion.1) | copy-start | bytes 3145732
  60.2 24.9 %collective-permute-start = (bf16[2048,256]{1,0:T(8,128)(2,1)S(1)}, bf16[2048,256]{1,0:T(8,128)(2,1)S(1)}, u32[]{:S(2)}, u32[]{:S(2)}) collective-permute-start(bf16[2048,256]{1,0:T(8,128)(2,1)S(1)} %bitcast.48), channel_id=1, source_target_pairs={{0,1},{1,2},{2,3},{3,0},{4,5},{5,6},{6,7},{7,4},{8,9},{9,10},{10,1... | collective-permute-start | bytes 3145736 | tf_op jit(solution)/shard_map/ppermute | solution.py:114
  61.5 24.7 %collective-permute-start.1 = (bf16[2048,256]{1,0:T(8,128)(2,1)S(1)}, bf16[2048,256]{1,0:T(8,128)(2,1)}, u32[]{:S(2)}, u32[]{:S(2)}) collective-permute-start(bf16[2048,256]{1,0:T(8,128)(2,1)S(1)} %bitcast.49), channel_id=1, source_target_pairs={{0,3},{1,0},{2,1},{3,2},{4,7},{5,4},{6,5},{7,6},{8,11},{9,8},{10,9... | collective-permute-start | bytes 3145736 | tf_op jit(solution)/shard_map/ppermute | solution.py:119
  85.1 24.0 %collective-permute-start.2 = (bf16[2048,256]{1,0:T(8,128)(2,1)S(1)}, bf16[2048,256]{1,0:T(8,128)(2,1)}, u32[]{:S(2)}, u32[]{:S(2)}) collective-permute-start(bf16[2048,256]{1,0:T(8,128)(2,1)S(1)} %collective-permute-done), channel_id=1, source_target_pairs={{0,1},{1,2},{2,3},{3,0},{4,5},{5,6},{6,7},{7,4},{8,9},{9,10},{10,1... | collective-permute-start | bytes 3145736 | tf_op jit(solution)/shard_map/ppermute | solution.py:114
  112.6 1.1 copy-start.6
  113.7 2.3 copy-start.7
  116.1 2.3 copy-start.8
  118.3 2.3 copy-start.4
  223.4 5.7 %copy-start.2 = (bf16[128,16,256]{2,1,0:T(8,128)(2,1)S(1)}, bf16[128,16,256]{2,1,0:T(8,128)(2,1)}, u32[]{:S(2)}) copy-start(bf16[128,16,256]{2,1,0:T(8,128)(2,1)} %copy-done.1) | copy-start | bytes 3145732
  223.4 51.1 %all-to-all-start.2 = ((bf16[4,2048,256]{1,2,0:T(8,128)(2,1)}), bf16[4,2048,256]{1,2,0:T(8,128)(2,1)}, u32[]{:S(2)}, u32[]{:S(2)}) async-start(bf16[4,2048,256]{1,2,0:T(8,128)(2,1)} %bitcast.47), calls=%async_computation.2 | async-start | bytes 8388608 | tf_op jit(solution)/shard_map/all_to_all | solution.py:19
  274.5 3.3 %copy-start.3 = (bf16[2048,256]{0,1:T(8,128)(2,1)S(1)}, bf16[2048,256]{0,1:T(8,128)(2,1)}, u32[]{:S(2)}) copy-start(bf16[2048,256]{0,1:T(8,128)(2,1)} %copy.23) | copy-start | bytes 3145732
  279.6 21.6 %all-to-all-start.3 = ((f32[64,1,257]{2,1,0:T(1,128)}), f32[64,1,257]{2,1,0:T(1,128)S(1)}, u32[]{:S(2)}, u32[]{:S(2)}) async-start(f32[64,1,257]{2,1,0:T(1,128)} %broadcast_in_dim.138), calls=%async_computation.3 | async-start | bytes 196608 | tf_op jit(solution)/shard_map/all_to_all | solution.py:25
